TPU v7x, 256 devices: a whole 4x4x8 slice. The times are simulated.
256 devices in a mesh: freq: 4 (over x_hi, core), rcv: 64 (over y, z, x_lo).
Axes of the slice: x: 4 (x_hi: 2, x_lo: 2; x = x_hi * 2 + x_lo), y: 4, z: 8, core: 2. Of those that a mesh axis runs over, the one named last changes fastest.
Arguments:
- reflection: bfloat16 [8, 2, 2560, 2560], P('freq', None, 'rcv'), may hold values from -5 to 5, as said below
- starts: int32 [2560, 192], P('rcv'), may hold values from 8 to 56
- focusing: float32 [8, 2560, 2, 192], P('freq', 'rcv'), may hold values from -6 to 6
- residual: float32 [8, 2560, 2, 192], P('freq', 'rcv'), may hold values from -6 to 6
- direction: float32 [8, 2560, 2, 192], P('freq', 'rcv'), may hold values from -6 to 6
- gradient: float32 [8, 2560, 2, 192], P('freq', 'rcv'), may hold values from -30 to 30
Outputs:
- new_focusing: float32 [8, 2560, 2, 192], P('freq', 'rcv')
- new_residual: float32 [8, 2560, 2, 192], P('freq', 'rcv')
- new_direction: float32 [8, 2560, 2, 192], P('freq', 'rcv')
- green_field: float32 [8, 2560, 2, 192], P('freq', 'rcv')
- focal_correlation: float32 [8, 2, 192], P('freq')
Inputs may be any that keep to these rules, and one draw needn't show every extreme that they name: Each frequency's matrix is symmetric in source and receiver: reflection[f, c, s, r] = reflection[f, c, r, s].
All inputs are finite; a program needn't handle non-finite values.
Results may differ from a plain program's by a relative error of at most 0.0003.
The roundings to bfloat16 on the way count: a program that leaves them out, or rounds other values in their place, can miss the bound.
Values may be sent and summed in bfloat16 or wider, within the bound.
A program may use at most 64 MiB of HBM per device.

v0:
```python
import math
import jax
import jax.numpy as jnp
from jax import lax
from jax.sharding import Mesh
from jax.sharding import PartitionSpec as P

N = 2560
F = 8
TS = 64
FREQ = ("freq_0", "freq_1")
RCV = ("rcv_0", "rcv_1", "rcv_2")
FREQ_RCV = ("freq_0", "freq_1", "rcv_0", "rcv_1", "rcv_2")
band_start = 5
tiny = 1e-06
highest = lax.Precision.HIGHEST


def in_order(pieces, dim):
    lengths = list(pieces.shape[1:])
    lengths[dim] *= pieces.shape[0]
    return jnp.moveaxis(pieces, 0, dim).reshape(lengths)


def sent_to_all(value, axis):
    count = lax.axis_size(axis)
    return lax.all_to_all(
        jnp.broadcast_to(value[None], (count, *value.shape)), axis, 0, 0, tiled=True
    )


def gather_directly(value, axis, dim):
    return in_order(sent_to_all(value, axis), dim)


def one_axis_at_a_time(value, axes):
    for axis in axes:
        value = lax.psum(value, axis)
    return value


def all_blocks(value, axes, sequence):
    pieces = value
    for k in sequence:
        pieces = lax.all_gather(pieces, axes[k])
    done = sequence[::-1]
    back = [done.index(k) for k in range(len(axes))]
    pieces = pieces.transpose(*back, *range(len(axes), pieces.ndim))
    return pieces.reshape(-1, *value.shape)


def gathered_by_axis(value, axes, sequence, dim):
    return in_order(all_blocks(value, axes, sequence), dim)


def of_everyone(value, axis):
    everything = sent_to_all(value, axis)
    return jnp.sum(everything, axis=0)


def tables(count, offset):
    times = jnp.arange(TS, dtype=jnp.float32)[:, None]
    bins = (jnp.arange(count, dtype=jnp.int32) + offset + band_start).astype(jnp.float32)[None, :]
    phase = 2.0 * jnp.pi * times * bins / TS
    return (jnp.cos(phase), jnp.sin(phase))


def contract_time(table, values):
    return jnp.einsum("tf,frk->trk", table, values, precision=highest)


def contract_back(table, values):
    return jnp.einsum("tf,trk->frk", table, values, precision=highest)


def time_gate(field, forward_cos, forward_sin, back_cos, back_sin, limits, complement):
    real_part = field[:, :, 0]
    imag_part = field[:, :, 1]
    time_real = contract_time(forward_cos, real_part) - contract_time(forward_sin, imag_part)
    time_imag = contract_time(forward_sin, real_part) + contract_time(forward_cos, imag_part)
    clock = jnp.arange(TS, dtype=jnp.int32)[:, None, None]
    window = (clock < limits[None]).astype(jnp.float32)
    if complement:
        window = 1.0 - window
    kept_real = window * time_real
    kept_imag = window * time_imag
    out_real = (contract_back(back_cos, kept_real) + contract_back(back_sin, kept_imag)) / TS
    out_imag = (contract_back(back_cos, kept_imag) - contract_back(back_sin, kept_real)) / TS
    return jnp.stack([out_real, out_imag], axis=2)


def combine(total, conjugate):
    if conjugate:
        out_real = total[:, 0, :, 0] + total[:, 1, :, 1]
        out_imag = total[:, 0, :, 1] - total[:, 1, :, 0]
    else:
        out_real = total[:, 0, :, 0] - total[:, 1, :, 1]
        out_imag = total[:, 0, :, 1] + total[:, 1, :, 0]
    return jnp.stack([out_real, out_imag], axis=2)


def per_device(reflection, starts, focusing, residual, direction, gradient):
    local_freq = reflection.shape[0]
    position = lax.axis_index(FREQ)
    cos_table, sin_table = tables(F, 0)
    own_cos, own_sin = tables(local_freq, position * local_freq)

    def gate(field, complement):
        whole = gather_directly(field, FREQ, 0)
        return time_gate(whole, cos_table, sin_table, own_cos, own_sin, starts, complement)

    def accumulate(piece):
        return jnp.einsum("fpnm,fmqk->fpnqk", reflection, piece, preferred_element_type=jnp.float32)

    direction_low = direction.astype(jnp.bfloat16)
    focusing_low = focusing.astype(jnp.bfloat16)
    aimed_total = accumulate(lax.all_gather(direction_low, RCV, axis=1, tiled=True))
    direction_image = combine(aimed_total, False)
    image = gate(direction_image, False)
    gamma, curvature = (
        one_axis_at_a_time(jnp.sum(gradient * gradient), FREQ_RCV),
        one_axis_at_a_time(jnp.sum(image * image), FREQ_RCV),
    )
    alpha = gamma / (curvature + tiny)
    new_focusing = focusing + alpha * direction
    new_residual = residual - alpha * image
    gated = gate(new_residual, False).astype(jnp.bfloat16)
    total = accumulate(gathered_by_axis(gated, RCV, (2, 0, 1), 1))
    new_gradient = combine(total, True)
    new_gamma = one_axis_at_a_time(jnp.sum(new_gradient * new_gradient), FREQ_RCV)
    new_direction = new_gradient + new_gamma / (gamma + tiny) * direction
    focus_total = accumulate(lax.all_gather(focusing_low, RCV, axis=1, tiled=True))
    focusing_image = combine(focus_total, False)
    green_field = gate(focusing_image + alpha * direction_image, True)
    corr_real = jnp.sum(
        green_field[:, :, 0] * new_focusing[:, :, 0] + green_field[:, :, 1] * new_focusing[:, :, 1],
        axis=1,
    )
    corr_imag = jnp.sum(
        green_field[:, :, 1] * new_focusing[:, :, 0] - green_field[:, :, 0] * new_focusing[:, :, 1],
        axis=1,
    )
    partial_corr = jnp.stack([corr_real, corr_imag], axis=1)
    focal_correlation = of_everyone(partial_corr, RCV) / math.sqrt(N)
    return (new_focusing, new_residual, new_direction, green_field, focal_correlation)


def solution(mesh):
    finer = Mesh(
        mesh.devices.reshape(2, 2, 4, 8, 2), ("freq_0", "freq_1", "rcv_0", "rcv_1", "rcv_2")
    )
    in_specs = (
        P(FREQ, None, RCV, None),
        P(RCV, None),
        P(FREQ, RCV, None, None),
        P(FREQ, RCV, None, None),
        P(FREQ, RCV, None, None),
        P(FREQ, RCV, None, None),
    )
    out_specs = (
        P(FREQ, RCV, None, None),
        P(FREQ, RCV, None, None),
        P(FREQ, RCV, None, None),
        P(FREQ, RCV, None, None),
        P(FREQ, None, None),
    )
    return jax.shard_map(
        per_device, mesh=finer, in_specs=in_specs, out_specs=out_specs, check_vma=False
    )
```

profile of v0, /device:TPU:4, one launch (start us, length us, event | category | flops | bytes accessed | tf_op | source)
XLA Modules:
  0.0 782.8 jit_solution(11673476122548457123)
XLA Ops:
  10.5 307.9 %all-gather.6.cloned.1.call-done = bf16[2,2560,2,192]{3,1,2,0:T(8,128)(2,1)} async-done(((bf16[2,40,2,192]{3,1,2,0:T(8,128)(2,1)}), bf16[2,2560,2,192]{3,1,2,0:T(8,128)(2,1)}) %all-gather.6.cloned.1.call-update) | async-done | bytes 3932176 | tf_op jit(solution)/shard_map/all_gather | solution.py:117
  318.5 3.5 fusion
  323.2 4.8 all-to-all-start
  328.8 12.3 %all-to-all-done = f32[4,2,40,2,192]{4,1,2,3,0:T(2,128)S(1)} async-done(((f32[4,2,40,2,192]{4,1,2,3,0:T(2,128)}), f32[4,2,40,2,192]{4,1,2,3,0:T(2,128)S(1)}, u32[]{:S(2)}, u32[]{:S(2)}) %all-to-all-start) | async-done | bytes 491552 | tf_op jit(solution)/shard_map/all_to_all | solution.py:27
  358.0 7.1 all-reduce.4
  365.1 3.1 all-reduce.3
  368.1 8.3 %all-reduce.1 = (f32[]{:T(128)}, f32[]{:T(128)}) all-reduce(f32[]{:T(128)} %get-tuple-element.38, f32[]{:T(128)} %get-tuple-element.39), channel_id=1, replica_groups=mesh['freq_0'=2,'freq_1'=2,'rcv_0'=4,'rcv_1'=8,'rcv_2'=2] {'rcv_0'}, use_global_device_ids=true, to_apply=%region_3.0 | all-reduce | flops 2 | bytes 16 | tf_op jit(solution)/shard_map/psum | solution.py:38
  376.5 20.8 %all-reduce = (f32[]{:T(128)}, f32[]{:T(128)}) all-reduce(f32[]{:T(128)} %get-tuple-element.34, f32[]{:T(128)} %get-tuple-element.35), channel_id=1, replica_groups=mesh['freq_0'=2,'freq_1'=2,'rcv_0'=4,'rcv_1'=8,'rcv_2'=2] {'rcv_1'}, use_global_device_ids=true, to_apply=%region_4.0 | all-reduce | flops 2 | bytes 16 | tf_op jit(solution)/shard_map/psum | solution.py:38
  397.3 5.8 all-reduce.2
  405.4 18.5 %all_to_all.20 = f32[4,2,40,2,192]{4,1,2,3,0:T(2,128)S(1)} all-to-all(f32[4,2,40,2,192]{4,1,2,3,0:T(2,128)S(1)} %broadcast_in_dim.9), channel_id=1, replica_groups=mesh['freq_0'=2,'freq_1'=2,'rcv_0'=4,'rcv_1'=8,'rcv_2'=2] {'freq_0','fre..., dimensions={0} | all-to-all | bytes 983040 | tf_op jit(solution)/shard_map/all_to_all | solution.py:27
  427.0 2.5 subtract_select_fusion
  433.3 2.5 add_select_fusion
  440.4 6.1 all_gather.23
  446.6 15.6 %all-gather = bf16[8,2,40,2,192]{4,2,3,1,0:T(8,128)(2,1)} all-gather(bf16[2,2,40,2,192]{4,2,3,1,0:T(8,128)(2,1)S(1)} %all_gather.23), channel_id=2, replica_groups=mesh['freq_0'=2,'freq_1'=2,'rcv_0'=4,'rcv_1'=8,'rcv_2'=2] {'rcv_0'}, dimensions={0}, use_global_device_ids=true | all-gather | bytes 614400 | tf_op jit(solution)/shard_map/all_gather | solution.py:45
  462.2 162.9 %all-gather.8.cloned.1.call-done = bf16[2,2560,2,192]{3,1,2,0:T(8,128)(2,1)} async-done(((bf16[2,40,2,192]{3,1,2,0:T(8,128)(2,1)}), bf16[2,2560,2,192]{3,1,2,0:T(8,128)(2,1)}) %all-gather.8.cloned.1.call-update) | async-done | bytes 3932176 | tf_op jit(solution)/shard_map/all_gather | solution.py:132
  625.1 3.5 fusion.2
  629.8 4.8 all-to-all-start.2
  635.3 7.9 %all-to-all-done.2 = f32[4,2,40,2,192]{4,1,2,3,0:T(2,128)S(1)} async-done(((f32[4,2,40,2,192]{4,1,2,3,0:T(2,128)}), f32[4,2,40,2,192]{4,1,2,3,0:T(2,128)S(1)}, u32[]{:S(2)}, u32[]{:S(2)}) %all-to-all-start.2) | async-done | bytes 491552 | tf_op jit(solution)/shard_map/all_to_all | solution.py:27
  646.3 3.9 fusion.12
  650.1 3.7 add_multiply_fusion
  653.8 34.5 %all-gather.10.cloned.1.call-done = bf16[32,2,2,40,2,192]{5,3,4,2,1,0:T(8,128)(2,1)} async-done(((bf16[4,2,2,40,2,192]{5,3,4,2,1,0:T(8,128)(2,1)}), bf16[32,2,2,40,2,192]{5,3,4,2,1,0:T(8,128)(2,1)}) %all-gather.10.cloned.1.call-update) | async-done | bytes 3932176 | tf_op jit(solution)/shard_map/all_gather | solution.py:45
  688.3 3.0 copy.180
  694.3 4.3 subtract_multiply_fusion
  698.6 7.1 psum.115
  705.7 3.8 fusion.109
  709.4 3.3 psum.116
  712.7 3.7 fusion.95
  716.4 11.1 %psum.117 = f32[]{:T(128)} all-reduce(f32[]{:T(128)} %psum.116), channel_id=1, replica_groups=mesh['freq_0'=2,'freq_1'=2,'rcv_0'=4,'rcv_1'=8,'rcv_2'=2] {'rcv_0'}, use_global_device_ids=true, to_apply=%region_15.0 | all-reduce | flops 1 | bytes 8 | tf_op jit(solution)/shard_map/psum | solution.py:38
  729.5 16.1 %psum.118 = f32[]{:T(128)} all-reduce(f32[]{:T(128)} %psum.117), channel_id=1, replica_groups=mesh['freq_0'=2,'freq_1'=2,'rcv_0'=4,'rcv_1'=8,'rcv_2'=2] {'rcv_1'}, use_global_device_ids=true, to_apply=%region_16.0 | all-reduce | flops 1 | bytes 8 | tf_op jit(solution)/shard_map/psum | solution.py:38
  747.7 5.5 psum.119
  756.9 7.5 all-to-all-start.3
  768.4 6.9 all-to-all-done.3
  (90 shorter events, 53.4 us)
Async XLA Ops:
  7.2 311.3 %copy-start = (bf16[2,2,40,2560]{3,2,1,0:T(8,128)(2,1)S(1)}, bf16[2,2,40,2560]{3,2,1,0:T(8,128)(2,1)}, u32[]{:S(2)}) copy-start(bf16[2,2,40,2560]{3,2,1,0:T(8,128)(2,1)} %param.6) | copy-start | bytes 2457604
  7.2 311.3 %all-gather.6.cloned.1.call-start = ((), (), s32[]{:S(2)}) async-start(), calls=%async_computation.4 | async-start | bytes 5324800 | tf_op jit(solution)/shard_map/all_gather | solution.py:117
  8.9 616.2 %all-gather.8.cloned.1.call-start = ((), (), s32[]{:S(2)}) async-start(), calls=%async_computation.5 | async-start | bytes 5324800 | tf_op jit(solution)/shard_map/all_gather | solution.py:132
  322.0 6.0 copy-start.8
  323.2 17.9 %all-to-all-start = ((f32[4,2,40,2,192]{4,1,2,3,0:T(2,128)}), f32[4,2,40,2,192]{4,1,2,3,0:T(2,128)S(1)}, u32[]{:S(2)}, u32[]{:S(2)}) async-start(f32[4,2,40,2,192]{4,1,2,3,0:T(2,128)} %broadcast_in_dim.8), calls=%async_computation | async-start | bytes 1310720 | tf_op jit(solution)/shard_map/all_to_all | solution.py:27
  328.0 360.4 %all-gather.10.cloned.1.call-start = ((), (), s32[]{:S(2)}) async-start(), calls=%async_computation.6 | async-start | bytes 5898240 | tf_op jit(solution)/shard_map/all_gather | solution.py:45
  328.8 15.4 %copy-start.4 = (s32[40,192]{1,0:T(8,128)S(1)}, s32[40,192]{1,0:T(8,128)}, u32[]{:S(2)}) copy-start(s32[40,192]{1,0:T(8,128)} %param.7) | copy-start | bytes 92164
  354.4 50.0 %copy-start.9 = (f32[2,40,2,192]{3,2,1,0:T(2,128)S(1)}, f32[2,40,2,192]{3,2,1,0:T(2,128)}, u32[]{:S(2)}) copy-start(f32[2,40,2,192]{3,2,1,0:T(2,128)} %param.9) | copy-start | bytes 368644
  404.4 0.7 copy-start.5
  629.8 13.4 %all-to-all-start.2 = ((f32[4,2,40,2,192]{4,1,2,3,0:T(2,128)}), f32[4,2,40,2,192]{4,1,2,3,0:T(2,128)S(1)}, u32[]{:S(2)}, u32[]{:S(2)}) async-start(f32[4,2,40,2,192]{4,1,2,3,0:T(2,128)} %broadcast_in_dim.10), calls=%async_computation.2 | async-start | bytes 1310720 | tf_op jit(solution)/shard_map/all_to_all | solution.py:27
  643.9 2.4 copy-start.2
  691.4 3.0 copy-start.1
  691.4 3.0 copy-start.3
  692.4 0.6 copy-start.6
  693.1 0.6 copy-start.7
  756.9 18.5 %all-to-all-start.3 = ((f32[64,2,2,192]{3,2,1,0:T(2,128)}), f32[64,2,2,192]{3,2,1,0:T(2,128)S(1)}, u32[]{:S(2)}, u32[]{:S(2)}) async-start(f32[64,2,2,192]{3,2,1,0:T(2,128)} %broadcast_in_dim.11), calls=%async_computation.3 | async-start | bytes 524288 | tf_op jit(solution)/shard_map/all_to_all | solution.py:27
Sparse Core Ops, SparseCore 0:
  10.4 308.0 all-gather.5
  320.8 304.2 all-gather.7
  626.9 61.3 all-gather.9
where the time goes:
time: 793 us; the launch traced here: 783 us
  waiting for transfers between devices  533 us (67%)
  blocking collectives  128 us (16%)
  matrix products  65.1 us (8%)
  local copies, waits for them, and re-layouts  17.5 us (2%)
  starting transfers between devices  17.1 us (2%)
  between operations  16.9 us (2%)
    all_gather x1, waiting for transfers between devices, per_device(): lax.all_gather(direction_low, RCV, axis=1, tiled=True)  308 us
    all_gather x1, waiting for transfers between devices, per_device(): lax.all_gather(focusing_low, RCV, axis=1, tiled=True)  163 us
    psum x10, blocking collectives, one_axis_at_a_time(): value = lax.psum(value, axis)  88.1 us
    all_gather x1, waiting for transfers between devices, all_blocks(): pieces = lax.all_gather(pieces, axes[k])  34.5 us
    dot_general x12, matrix products, contract_time(): return jnp.einsum('tf,frk->trk', table, values, precision=highest)  33.8 us
    all_to_all x3, waiting for transfers between devices, sent_to_all(): lax.all_to_all(jnp.broadcast_to(value[None], (count, *value.shape)), axis...  27.2 us
    dot_general x12, matrix products, contract_back(): return jnp.einsum('tf,trk->frk', table, values, precision=highest)  23.2 us
    all_gather x2, blocking collectives, all_blocks(): pieces = lax.all_gather(pieces, axes[k])  21.7 us
  transfers between devices with their start and end apart: 6, of which 6 were waited for; matrix products, arithmetic and copies ran while one was open for 8% of the time, Pallas kernels for 0%

commit v1 on v0

--- a/solution.py
+++ b/solution.py
@@ -14,6 +14,12 @@
 band_start = 5
 tiny = 1e-06
 highest = lax.Precision.HIGHEST
+
+
+def gathered_along(array, axis, d):
+    parts = lax.all_gather(array, axis, axis=0, tiled=False)
+    whole = jnp.concatenate(parts, axis=d)
+    return whole
 
 
 def in_order(pieces, dim):
@@ -114,7 +120,7 @@
 
     direction_low = direction.astype(jnp.bfloat16)
     focusing_low = focusing.astype(jnp.bfloat16)
-    aimed_total = accumulate(lax.all_gather(direction_low, RCV, axis=1, tiled=True))
+    aimed_total = accumulate(gathered_along(direction_low, RCV, 1))
     direction_image = combine(aimed_total, False)
     image = gate(direction_image, False)
     gamma, curvature = (

time: 793 us -> 792 us (level)
  no operation moved by 1% of the time
where the time goes in v1:
time: 792 us; the launch traced here: 781 us
  waiting for transfers between devices  531 us (67%)
  blocking collectives  128 us (16%)
  matrix products  62.6 us (8%)
  local copies, waits for them, and re-layouts  20.3 us (3%)
  starting transfers between devices  17.2 us (2%)
  between operations  16.9 us (2%)
    all_gather x1, waiting for transfers between devices, gathered_along(): parts = lax.all_gather(array, axis, axis=0, tiled=False)  308 us
    all_gather x1, waiting for transfers between devices, per_device(): lax.all_gather(focusing_low, RCV, axis=1, tiled=True)  162 us
    psum x10, blocking collectives, one_axis_at_a_time(): value = lax.psum(value, axis)  87.7 us
    all_gather x1, waiting for transfers between devices, all_blocks(): pieces = lax.all_gather(pieces, axes[k])  33.8 us
    dot_general x12, matrix products, contract_time(): return jnp.einsum('tf,frk->trk', table, values, precision=highest)  33.8 us
    all_to_all x3, waiting for transfers between devices, sent_to_all(): lax.all_to_all(jnp.broadcast_to(value[None], (count, *value.shape)), axis...  27.4 us
    dot_general x12, matrix products, contract_back(): return jnp.einsum('tf,trk->frk', table, values, precision=highest)  23.2 us
    all_gather x2, blocking collectives, all_blocks(): pieces = lax.all_gather(pieces, axes[k])  22.1 us
  transfers between devices with their start and end apart: 6, of which 6 were waited for; matrix products, arithmetic and copies ran while one was open for 8% of the time, Pallas kernels for 0%

profile of v1, /device:TPU:4, one launch (start us, length us, event | category | flops | bytes accessed | tf_op | source)
XLA Modules:
  0.0 781.4 jit_solution(5329306321623116794)
XLA Ops:
  10.5 308.0 %all-gather.9.cloned.1.call-done = bf16[128,40,2,192]{3,1,2,0:T(8,128)(2,1)} async-done(((bf16[2,40,2,192]{3,1,2,0:T(8,128)(2,1)}), bf16[128,40,2,192]{3,1,2,0:T(8,128)(2,1)}) %all-gather.9.cloned.1.call-update) | async-done | bytes 3932176 | tf_op jit(solution)/shard_map/all_gather | solution.py:20
  318.5 2.8 copy.167
  323.6 4.8 all-to-all-start
  329.2 12.5 %all-to-all-done = f32[4,2,40,2,192]{4,1,2,3,0:T(2,128)S(1)} async-done(((f32[4,2,40,2,192]{4,1,2,3,0:T(2,128)}), f32[4,2,40,2,192]{4,1,2,3,0:T(2,128)S(1)}, u32[]{:S(2)}, u32[]{:S(2)}) %all-to-all-start) | async-done | bytes 491552 | tf_op jit(solution)/shard_map/all_to_all | solution.py:33
  358.6 7.1 all-reduce.4
  365.6 3.1 all-reduce.3
  368.7 8.3 %all-reduce.1 = (f32[]{:T(128)}, f32[]{:T(128)}) all-reduce(f32[]{:T(128)} %get-tuple-element.38, f32[]{:T(128)} %get-tuple-element.39), channel_id=1, replica_groups=mesh['freq_0'=2,'freq_1'=2,'rcv_0'=4,'rcv_1'=8,'rcv_2'=2] {'rcv_0'}, use_global_device_ids=true, to_apply=%region_3.0 | all-reduce | flops 2 | bytes 16 | tf_op jit(solution)/shard_map/psum | solution.py:44
  377.1 20.4 %all-reduce = (f32[]{:T(128)}, f32[]{:T(128)}) all-reduce(f32[]{:T(128)} %get-tuple-element.34, f32[]{:T(128)} %get-tuple-element.35), channel_id=1, replica_groups=mesh['freq_0'=2,'freq_1'=2,'rcv_0'=4,'rcv_1'=8,'rcv_2'=2] {'rcv_1'}, use_global_device_ids=true, to_apply=%region_4.0 | all-reduce | flops 2 | bytes 16 | tf_op jit(solution)/shard_map/psum | solution.py:44
  397.5 5.8 all-reduce.2
  405.5 18.3 %all_to_all.20 = f32[4,2,40,2,192]{4,1,2,3,0:T(2,128)S(1)} all-to-all(f32[4,2,40,2,192]{4,1,2,3,0:T(2,128)S(1)} %broadcast_in_dim.9), channel_id=1, replica_groups=mesh['freq_0'=2,'freq_1'=2,'rcv_0'=4,'rcv_1'=8,'rcv_2'=2] {'freq_0','fre..., dimensions={0} | all-to-all | bytes 983040 | tf_op jit(solution)/shard_map/all_to_all | solution.py:33
  426.9 2.5 subtract_select_fusion
  433.2 2.5 add_select_fusion
  440.4 6.6 all_gather.27
  446.9 15.5 %all-gather.1 = bf16[8,2,40,2,192]{4,2,3,1,0:T(8,128)(2,1)} all-gather(bf16[2,2,40,2,192]{4,2,3,1,0:T(8,128)(2,1)S(1)} %all_gather.27), channel_id=3, replica_groups=mesh['freq_0'=2,'freq_1'=2,'rcv_0'=4,'rcv_1'=8,'rcv_2'=2] {'rcv_0'}, dimensions={0}, use_global_device_ids=true | all-gather | bytes 614400 | tf_op jit(solution)/shard_map/all_gather | solution.py:51
  462.5 161.8 %all-gather.7.cloned.1.call-done = bf16[2,2560,2,192]{3,1,2,0:T(8,128)(2,1)} async-done(((bf16[2,40,2,192]{3,1,2,0:T(8,128)(2,1)}), bf16[2,2560,2,192]{3,1,2,0:T(8,128)(2,1)}) %all-gather.7.cloned.1.call-update) | async-done | bytes 3932176 | tf_op jit(solution)/shard_map/all_gather | solution.py:138
  624.2 3.5 fusion
  629.0 4.8 all-to-all-start.2
  634.4 7.9 %all-to-all-done.2 = f32[4,2,40,2,192]{4,1,2,3,0:T(2,128)S(1)} async-done(((f32[4,2,40,2,192]{4,1,2,3,0:T(2,128)}), f32[4,2,40,2,192]{4,1,2,3,0:T(2,128)S(1)}, u32[]{:S(2)}, u32[]{:S(2)}) %all-to-all-start.2) | async-done | bytes 491552 | tf_op jit(solution)/shard_map/all_to_all | solution.py:33
  645.4 3.9 fusion.11
  649.3 3.7 add_multiply_fusion
  653.0 33.8 %all-gather.11.cloned.1.call-done = bf16[32,2,2,40,2,192]{5,3,4,2,1,0:T(8,128)(2,1)} async-done(((bf16[4,2,2,40,2,192]{5,3,4,2,1,0:T(8,128)(2,1)}), bf16[32,2,2,40,2,192]{5,3,4,2,1,0:T(8,128)(2,1)}) %all-gather.11.cloned.1.call-update) | async-done | bytes 3932176 | tf_op jit(solution)/shard_map/all_gather | solution.py:51
  686.8 3.0 copy.187
  692.8 4.3 subtract_multiply_fusion
  697.1 7.1 psum.115
  704.2 3.8 fusion.108
  707.9 3.3 psum.116
  711.2 3.7 fusion.94
  714.9 11.1 %psum.117 = f32[]{:T(128)} all-reduce(f32[]{:T(128)} %psum.116), channel_id=1, replica_groups=mesh['freq_0'=2,'freq_1'=2,'rcv_0'=4,'rcv_1'=8,'rcv_2'=2] {'rcv_0'}, use_global_device_ids=true, to_apply=%region_15.0 | all-reduce | flops 1 | bytes 8 | tf_op jit(solution)/shard_map/psum | solution.py:44
  728.0 16.1 %psum.118 = f32[]{:T(128)} all-reduce(f32[]{:T(128)} %psum.117), channel_id=1, replica_groups=mesh['freq_0'=2,'freq_1'=2,'rcv_0'=4,'rcv_1'=8,'rcv_2'=2] {'rcv_1'}, use_global_device_ids=true, to_apply=%region_16.0 | all-reduce | flops 1 | bytes 8 | tf_op jit(solution)/shard_map/psum | solution.py:44
  746.2 5.5 psum.119
  755.4 7.5 all-to-all-start.3
  767.0 6.9 all-to-all-done.3
  (91 shorter events, 54.4 us)
Async XLA Ops:
  7.2 314.2 %copy-start = (bf16[2,2,40,2560]{3,2,1,0:T(8,128)(2,1)S(1)}, bf16[2,2,40,2560]{3,2,1,0:T(8,128)(2,1)}, u32[]{:S(2)}) copy-start(bf16[2,2,40,2560]{3,2,1,0:T(8,128)(2,1)} %param.6) | copy-start | bytes 2457604
  7.2 311.3 %all-gather.9.cloned.1.call-start = ((), (), s32[]{:S(2)}) async-start(), calls=%async_computation.5 | async-start | bytes 5324800 | tf_op jit(solution)/shard_map/all_gather | solution.py:20
  8.9 615.4 %all-gather.7.cloned.1.call-start = ((), (), s32[]{:S(2)}) async-start(), calls=%async_computation.4 | async-start | bytes 5324800 | tf_op jit(solution)/shard_map/all_gather | solution.py:138
  322.4 6.0 copy-start.8
  323.6 18.1 %all-to-all-start = ((f32[4,2,40,2,192]{4,1,2,3,0:T(2,128)}), f32[4,2,40,2,192]{4,1,2,3,0:T(2,128)S(1)}, u32[]{:S(2)}, u32[]{:S(2)}) async-start(f32[4,2,40,2,192]{4,1,2,3,0:T(2,128)} %broadcast_in_dim.8), calls=%async_computation | async-start | bytes 1310720 | tf_op jit(solution)/shard_map/all_to_all | solution.py:33
  328.4 358.4 %all-gather.11.cloned.1.call-start = ((), (), s32[]{:S(2)}) async-start(), calls=%async_computation.6 | async-start | bytes 5898240 | tf_op jit(solution)/shard_map/all_gather | solution.py:51
  329.2 15.6 %copy-start.4 = (s32[40,192]{1,0:T(8,128)S(1)}, s32[40,192]{1,0:T(8,128)}, u32[]{:S(2)}) copy-start(s32[40,192]{1,0:T(8,128)} %param.7) | copy-start | bytes 92164
  354.9 49.6 %copy-start.9 = (f32[2,40,2,192]{3,2,1,0:T(2,128)S(1)}, f32[2,40,2,192]{3,2,1,0:T(2,128)}, u32[]{:S(2)}) copy-start(f32[2,40,2,192]{3,2,1,0:T(2,128)} %param.9) | copy-start | bytes 368644
  404.6 0.7 copy-start.5
  629.0 13.4 %all-to-all-start.2 = ((f32[4,2,40,2,192]{4,1,2,3,0:T(2,128)}), f32[4,2,40,2,192]{4,1,2,3,0:T(2,128)S(1)}, u32[]{:S(2)}, u32[]{:S(2)}) async-start(f32[4,2,40,2,192]{4,1,2,3,0:T(2,128)} %broadcast_in_dim.10), calls=%async_computation.2 | async-start | bytes 1310720 | tf_op jit(solution)/shard_map/all_to_all | solution.py:33
  643.0 2.4 copy-start.2
  689.8 3.0 copy-start.1
  689.8 3.0 copy-start.3
  690.9 0.6 copy-start.6
  691.5 0.6 copy-start.7
  755.4 18.6 %all-to-all-start.3 = ((f32[64,2,2,192]{3,2,1,0:T(2,128)}), f32[64,2,2,192]{3,2,1,0:T(2,128)S(1)}, u32[]{:S(2)}, u32[]{:S(2)}) async-start(f32[64,2,2,192]{3,2,1,0:T(2,128)} %broadcast_in_dim.11), calls=%async_computation.3 | async-start | bytes 524288 | tf_op jit(solution)/shard_map/all_to_all | solution.py:33
Sparse Core Ops, SparseCore 0:
  10.3 308.1 all-gather.8
  320.9 303.3 all-gather.6
  626.0 60.7 all-gather.10
